TPU v7x, 256 devices: a 4x2x16 block of a 4x16x16 slice. The times are simulated.
256 devices in a mesh: groups: 2 (over y), tp: 16 (over z), tq: 4 (over x), tr: 2 (over core).
Axes of the slice: x: 4, y: 2, z: 16, core: 2. Of those that a mesh axis runs over, the one named last changes fastest.
The devices are a block of a 4x16x16 slice.
Arguments:
- attn_heads: bfloat16 [128, 16384], P('groups', ('tp', 'tq', 'tr')), parts along dimension 0, may hold values from -6 to 6
- residual: bfloat16 [128, 16384], P('groups', ('tp', 'tq', 'tr')), parts along dimension 0, may hold values from -120 to 120
- o_weight: bfloat16 [16384, 16384], P(('tp', 'tq', 'tr')), may hold values from -0.1875 to 0.1875
- norm_gain: bfloat16 [16384], P(('tp', 'tq', 'tr')), may hold values from 0.099609375 to 1.8984375
- q_weight: bfloat16 [16384, 16384], P(None, ('tp', 'tq', 'tr')), may hold values from -0.046875 to 0.046875
Outputs:
- hidden: bfloat16 [128, 16384], P('groups', ('tp', 'tq', 'tr')), parts along dimension 0
- peak_value: float32 [128], P('groups'), parts along dimension 0
- query: bfloat16 [128, 16384], P('groups', ('tp', 'tq', 'tr')), parts along dimension 0
There are 2 independent parts, one for each index of `groups`. A program takes and returns all parts, laid end to end along the dimension named above; an argument that names none is the same for every part. Nothing has to cross between parts.
All inputs are finite; a program needn't handle non-finite values. Where the computation divides by a largest or mean magnitude, that divisor is 1e-20 or more.
Results may differ from a plain program's by a relative error of at most 0.0095.
Values may be sent and summed in bfloat16 or wider, within the bound.
No kernel may reach another device: no remote copies, remote signals or barrier semaphores. Data moves between devices by JAX's collectives and lax.ppermute only.
A program may use at most 64 MiB of HBM per device.

v0:
```python
import jax
import jax.numpy as jnp
from jax import lax
from jax.sharding import PartitionSpec as P

D = 16384


def in_blocks(array, dim, devices):
    dims = array.shape
    tiles = array.reshape(*dims[:dim], devices, dims[dim] // devices, *dims[dim + 1 :])
    return jnp.moveaxis(tiles, dim, 0)


def summed_on_arrival(array, axis, dim):
    tiles = in_blocks(array, dim, lax.axis_size(axis))
    arrived = lax.all_to_all(tiles, axis, split_axis=0, concat_axis=0, tiled=True)
    return arrived.sum(axis=0)


def collected_together(array, axis):
    leaves = jax.tree.leaves(array)
    turns = sorted(range(len(leaves)), key=lambda k: -leaves[k].size)
    width = (1, *leaves[turns[0]].shape)[-1]
    lines = [
        jnp.pad(leaves[k].reshape(-1), (0, -leaves[k].size % width)).reshape(-1, width)
        for k in turns
    ]
    both, at, found = (lax.all_gather(jnp.concatenate(lines), axis), 0, {})
    for k, line in zip(turns, lines):
        share = both[:, at : at + len(line)].reshape(len(both), -1)
        found[k] = share[:, : leaves[k].size].reshape(-1, *leaves[k].shape)
        at += len(line)
    numbers = iter(range(len(leaves)))
    return jax.tree.map(lambda _: found[next(numbers)], array)


def joined_all(array, axes, combine):
    for axis in axes:
        pieces = collected_together(array, axis)
        array = jax.tree.map(lambda part: part[0], pieces)
        for k in range(1, lax.axis_size(axis)):
            array = combine(array, jax.tree.map(lambda part: part[k], pieces))
    return array


def laid_out(tiles, dim):
    tiles = jnp.moveaxis(tiles, 0, dim)
    dims = tiles.shape
    return tiles.reshape(*dims[:dim], dims[dim] * dims[dim + 1], *dims[dim + 2 :])


def from_everyone(array, axis):
    copies = jnp.broadcast_to(array, (lax.axis_size(axis), *array.shape))
    return lax.all_to_all(copies, axis, split_axis=0, concat_axis=0, tiled=True)


def collect(array, axis, dim):
    return laid_out(from_everyone(array, axis), dim)


def combine_stats(lhs_stats, rhs_stats):
    return (lhs_stats[0] + rhs_stats[0], jnp.maximum(lhs_stats[1], rhs_stats[1]))


def body(attn_heads, residual, o_weight, norm_gain, q_weight):
    terms = jnp.dot(attn_heads, o_weight, preferred_element_type=jnp.float32)
    section_one = lax.psum_scatter(terms, "tp", scatter_dimension=1, tiled=True)
    section_two = summed_on_arrival(section_one, "tq", 1)
    attn_total = summed_on_arrival(section_two, "tr", 1)
    hidden = (residual.astype(jnp.float32) + attn_total).astype(jnp.bfloat16)
    widened = hidden.astype(jnp.float32)
    gained = widened * norm_gain.astype(jnp.float32)
    squares = jnp.sum(widened * widened, axis=1)
    local_top = jnp.max(jnp.abs(gained), axis=1)
    row_total, global_top = joined_all((squares, local_top), ("tp", "tq", "tr"), combine_stats)
    inv_rms = lax.rsqrt(row_total / D + 1e-05)
    normed = gained * inv_rms[:, None]
    peak_value = global_top * inv_rms
    quantized = (normed * (448.0 / (peak_value + 1e-06))[:, None]).astype(jnp.bfloat16)
    gathered_two = collect(quantized, "tr", 1)
    gathered_four = collect(gathered_two, "tq", 1)
    projected = jnp.dot(
        lax.all_gather(gathered_four, "tp", axis=1, tiled=True),
        q_weight,
        preferred_element_type=jnp.float32,
    )
    query = (projected * ((peak_value + 1e-06) / 448.0)[:, None]).astype(jnp.bfloat16)
    return (hidden, peak_value, query)


def solution(mesh):
    placed = (
        P("groups", ("tp", "tq", "tr")),
        P("groups", ("tp", "tq", "tr")),
        P(("tp", "tq", "tr"), None),
        P(("tp", "tq", "tr")),
        P(None, ("tp", "tq", "tr")),
    )
    return jax.shard_map(
        body,
        mesh=mesh,
        in_specs=placed,
        out_specs=(P("groups", ("tp", "tq", "tr")), P("groups"), P("groups", ("tp", "tq", "tr"))),
        check_vma=False,
    )
```

profile of v0, /device:TPU:34, one launch (start us, length us, event | category | flops | bytes accessed | tf_op | source)
XLA Modules:
  0.0 252.2 jit_solution(817903353825983854)
XLA Ops:
  7.2 0.0 copy-start
  7.2 0.1 reduce-scatter.2.cloned.1.call-start
  7.3 0.6 copy-done
  7.9 4.8 %fusion.15 = f32[64,16384]{1,0:T(8,128)} fusion(bf16[64,128]{1,0:T(8,128)(2,1)S(1)} %copy-done, bf16[128,16384]{1,0:T(8,128)(2,1)} %param.7), kind=kOutput, calls=%fused_computation.64 | convolution fusion | flops 268435456 | bytes 8404992 | tf_op jit(solution)/shard_map/dot_general | solution.py:67
  12.7 0.0 copy-start.4
  12.7 0.0 copy-start.2
  12.7 0.1 reduce-scatter.2.cloned.1.call-update
  12.8 92.7 %reduce-scatter.2.cloned.1.call-done = f32[64,1024]{1,0:T(8,128)} async-done(((f32[64,16384]{1,0:T(8,128)}), f32[64,1024]{1,0:T(8,128)}) %reduce-scatter.2.cloned.1.call-update) | async-done | bytes 262160 | tf_op jit(solution)/shard_map/reduce_scatter | solution.py:68
  105.5 1.7 copy.20
  107.1 5.0 %all-to-all-start = ((f32[4,64,256]{2,1,0:T(8,128)}), f32[4,64,256]{2,1,0:T(8,128)S(1)}, u32[]{:S(2)}, u32[]{:S(2)}) async-start(f32[4,64,256]{2,1,0:T(8,128)} %bitcast.44), calls=%async_computation.1 | async-start | bytes 524288 | tf_op jit(solution)/shard_map/all_to_all | solution.py:17
  112.2 0.0 all-gather.8.cloned.1.call-start
  112.2 0.0 copy-done.4
  112.2 5.2 %all-to-all-done = f32[4,64,256]{2,1,0:T(8,128)S(1)} async-done(((f32[4,64,256]{2,1,0:T(8,128)}), f32[4,64,256]{2,1,0:T(8,128)S(1)}, u32[]{:S(2)}, u32[]{:S(2)}) %all-to-all-start) | async-done | bytes 262176 | tf_op jit(solution)/shard_map/all_to_all | solution.py:17
  117.5 3.8 %all_to_all.20 = f32[2,64,128]{2,1,0:T(8,128)S(1)} all-to-all(f32[2,64,128]{2,1,0:T(8,128)S(1)} %copy.12), channel_id=1, replica_groups=mesh['groups'=2,'tp'=16,'tq'=4,'tr'=2] {'tr'}, dimensions={0} | all-to-all | bytes 131072 | tf_op jit(solution)/shard_map/all_to_all | solution.py:17
  121.3 0.0 copy-done.2
  121.3 0.1 fusion.6
  121.4 0.0 copy-start.1
  121.4 27.3 %all-gather.3 = f32[16,2,64]{2,1,0:T(2,128)S(1)} all-gather(f32[1,2,64]{2,1,0:T(2,128)S(1)} %maximum_bitcast_fusion), channel_id=2, replica_groups=mesh['groups'=2,'tp'=16,'tq'=4,'tr'=2] {'tp'}, dimensions={0}, use_global_device_ids=true | all-gather | bytes 8704 | tf_op jit(solution)/shard_map/all_gather | solution.py:29
  148.7 8.5 %all-gather.4 = f32[4,2,64]{2,1,0:T(2,128)S(1)} all-gather(f32[1,2,64]{2,1,0:T(2,128)S(1)} %maximum_bitcast_fusion.1), channel_id=3, replica_groups=mesh['groups'=2,'tp'=16,'tq'=4,'tr'=2] {'tq'}, dimensions={0}, use_global_device_ids=true | all-gather | bytes 2560 | tf_op jit(solution)/shard_map/all_gather | solution.py:29
  157.3 1.9 all-gather.5
  159.1 0.0 copy-start.3
  159.2 0.1 fusion.5
  159.3 3.8 %all_to_all.21 = bf16[2,64,128]{2,1,0:T(8,128)(2,1)S(1)} all-to-all(bf16[2,64,128]{2,1,0:T(8,128)(2,1)S(1)} %broadcast_in_dim.4), channel_id=1, replica_groups=mesh['groups'=2,'tp'=16,'tq'=4,'tr'=2] {'tr'}, dimensions={0} | all-to-all | bytes 65536 | tf_op jit(solution)/shard_map/all_to_all | solution.py:55
  163.0 8.1 %all_to_all.22 = bf16[4,64,256]{2,1,0:T(8,128)(2,1)S(1)} all-to-all(bf16[4,64,256]{2,1,0:T(8,128)(2,1)S(1)} %broadcast_in_dim.5), channel_id=1, replica_groups=mesh['groups'=2,'tp'=16,'tq'=4,'tr'=2] {'tq'}, dimensions={0} | all-to-all | bytes 262144 | tf_op jit(solution)/shard_map/all_to_all | solution.py:55
  171.1 0.7 copy.17
  171.8 0.1 all-gather.8.cloned.1.call-update
  171.9 69.2 %all-gather.8.cloned.1.call-done = bf16[64,16384]{1,0:T(8,128)(2,1)} async-done(((bf16[64,1024]{1,0:T(8,128)(2,1)}), bf16[64,16384]{1,0:T(8,128)(2,1)}) %all-gather.8.cloned.1.call-update) | async-done | bytes 2097168 | tf_op jit(solution)/shard_map/all_gather | solution.py:84
  241.1 4.3 %fusion = bf16[64,128]{1,0:T(8,128)(2,1)} fusion(bf16[64,16384]{1,0:T(8,128)(2,1)} %all-gather.8.cloned.1.call-done, bf16[16384,128]{1,0:T(8,128)(2,1)} %param.9, f32[64]{0:T(128)S(1)} %get-tuple-element.5), kind=kOutput, calls=%fused_computation.1 | convolution fusion | flops 268451840 | bytes 6308096 | tf_op jit(solution)/shard_map/dot_general | solution.py:83
  245.3 0.0 copy-done.1
  245.3 0.0 copy-done.3
  (16 shorter events, 0.2 us)
Async XLA Ops:
  7.2 0.7 copy-start
  7.2 98.3 %reduce-scatter.2.cloned.1.call-start = ((), (), s32[]{:S(2)}) async-start(), calls=%async_computation.5 | async-start | bytes 4456448 | tf_op jit(solution)/shard_map/reduce_scatter | solution.py:68
  12.7 99.4 %copy-start.4 = (bf16[128]{0:T(256)(128)(2,1)S(1)}, bf16[128]{0:T(256)(128)(2,1)}, u32[]{:S(2)}) copy-start(bf16[128]{0:T(256)(128)(2,1)} %param.8) | copy-start | bytes 772
  12.7 108.5 %copy-start.2 = (bf16[64,128]{1,0:T(8,128)(2,1)S(1)}, bf16[64,128]{1,0:T(8,128)(2,1)}, u32[]{:S(2)}) copy-start(bf16[64,128]{1,0:T(8,128)(2,1)} %param.6) | copy-start | bytes 49156
  107.1 10.3 %all-to-all-start = ((f32[4,64,256]{2,1,0:T(8,128)}), f32[4,64,256]{2,1,0:T(8,128)S(1)}, u32[]{:S(2)}, u32[]{:S(2)}) async-start(f32[4,64,256]{2,1,0:T(8,128)} %bitcast.44), calls=%async_computation.1 | async-start | bytes 524288 | tf_op jit(solution)/shard_map/all_to_all | solution.py:17
  112.2 128.9 %all-gather.8.cloned.1.call-start = ((), (), s32[]{:S(2)}) async-start(), calls=%async_computation.6 | async-start | bytes 2228224 | tf_op jit(solution)/shard_map/all_gather | solution.py:84
  121.4 124.0 %copy-start.1 = (bf16[64,128]{1,0:T(8,128)(2,1)}, bf16[64,128]{1,0:T(8,128)(2,1)S(1)}, u32[]{:S(2)}) copy-start(bf16[64,128]{1,0:T(8,128)(2,1)S(1)} %get-tuple-element.8) | copy-start | bytes 49156
  159.1 86.2 %copy-start.3 = (f32[64]{0:T(128)}, f32[64]{0:T(128)S(1)}, u32[]{:S(2)}) copy-start(f32[64]{0:T(128)S(1)} %get-tuple-element.6) | copy-start | bytes 772
Sparse Core Ops, SparseCore 0:
  12.9 92.5 reduce-scatter.1
  172.0 69.0 all-gather.7
where the time goes:
time: 253 us; the launch traced here: 252 us
  waiting for transfers between devices  167 us (66%)
  blocking collectives  53.3 us (21%)
  between operations  14.2 us (6%)
  matrix products  9.1 us (4%)
  starting transfers between devices  5.09 us (2%)
  local copies, waits for them, and re-layouts  3.06 us (1%)
    reduce_scatter x1, waiting for transfers between devices, body(): section_one = lax.psum_scatter(terms, 'tp', scatter_dimension=1, tiled=True)  92.7 us
    all_gather x1, waiting for transfers between devices, body(): lax.all_gather(gathered_four, 'tp', axis=1, tiled=True)  69.2 us
    all_gather x3, blocking collectives, collected_together(): both, at, found = (lax.all_gather(jnp.concatenate(lines), axis), 0, {})  37.6 us
    all_to_all x2, blocking collectives, from_everyone(): return lax.all_to_all(copies, axis, split_axis=0, concat_axis=0, tiled=True)  11.9 us
    all_to_all x1, waiting for transfers between devices, summed_on_arrival(): lax.all_to_all(tiles, axis, split_axis=0, concat_axis=0, tiled=True)  5.21 us
  transfers between devices with their start and end apart: 3, of which 3 were waited for; matrix products, arithmetic and copies ran while one was open for 0% of the time, Pallas kernels for 0%

commit v1 on v0

--- a/solution.py
+++ b/solution.py
@@ -81,7 +81,9 @@
     gathered_two = collect(quantized, "tr", 1)
     gathered_four = collect(gathered_two, "tq", 1)
     projected = jnp.dot(
-        lax.all_gather(gathered_four, "tp", axis=1, tiled=True),
+        jnp.concatenate(
+            lax.all_to_all(jnp.stack([gathered_four] * lax.axis_size("tp")), "tp", 0, 0), axis=1
+        ),
         q_weight,
         preferred_element_type=jnp.float32,
     )

time: 253 us -> 286 us (1.13)
  blocking collectives: 53.3 us -> 159 us
  waiting for transfers between devices: 167 us -> 97.9 us
    all_to_all x0 -> x1, blocking collectives: none -> 106 us  [body(): lax.all_to_all(jnp.stack([gathered_four] * lax.axis_size('tp')), 'tp', 0, 0)]
    all_gather x1 -> x0, waiting for transfers between devices: 69.2 us -> none  [body(): lax.all_gather(gathered_four, 'tp', axis=1, tiled=True)]
  transfers between devices with their start and end apart: 3 -> 2, of which waited for: 3 -> 2; matrix products, arithmetic and copies ran while one was open for 0% -> 0% of each run, Pallas kernels for 0% -> 0%
where the time goes in v1:
time: 286 us
  blocking collectives  159 us (56%)
  waiting for transfers between devices  97.9 us (34%)
  between operations  14.2 us (5%)
  matrix products  6.28 us (2%)
  starting transfers between devices  5.09 us (2%)
  local copies, waits for them, and re-layouts  2.9 us (1%)
    all_to_all x1, blocking collectives, body(): lax.all_to_all(jnp.stack([gathered_four] * lax.axis_size('tp')), 'tp', 0, 0)  106 us
    reduce_scatter x1, waiting for transfers between devices, body(): section_one = lax.psum_scatter(terms, 'tp', scatter_dimension=1, tiled=True)  92.7 us
    all_gather x3, blocking collectives, collected_together(): both, at, found = (lax.all_gather(jnp.concatenate(lines), axis), 0, {})  37.6 us
    all_to_all x2, blocking collectives, from_everyone(): return lax.all_to_all(copies, axis, split_axis=0, concat_axis=0, tiled=True)  11.9 us
  transfers between devices with their start and end apart: 2, of which 2 were waited for; matrix products, arithmetic and copies ran while one was open for 0% of the time, Pallas kernels for 0%

profile of v1, /device:TPU:34, one launch (start us, length us, event | category | flops | bytes accessed | tf_op | source)
XLA Modules:
  0.0 285.6 jit_solution(1174764520111062832)
XLA Ops:
  7.2 0.0 copy-start
  7.2 0.1 reduce-scatter.2.cloned.1.call-start
  7.3 0.6 copy-done
  7.9 4.8 %fusion.15 = f32[64,16384]{1,0:T(8,128)} fusion(bf16[64,128]{1,0:T(8,128)(2,1)S(1)} %copy-done, bf16[128,16384]{1,0:T(8,128)(2,1)} %param.7), kind=kOutput, calls=%fused_computation.64 | convolution fusion | flops 268435456 | bytes 8404992 | tf_op jit(solution)/shard_map/dot_general | solution.py:67
  12.7 0.0 copy-start.5
  12.7 0.0 copy-start.3
  12.7 0.1 reduce-scatter.2.cloned.1.call-update
  12.8 92.7 %reduce-scatter.2.cloned.1.call-done = f32[64,1024]{1,0:T(8,128)} async-done(((f32[64,16384]{1,0:T(8,128)}), f32[64,1024]{1,0:T(8,128)}) %reduce-scatter.2.cloned.1.call-update) | async-done | bytes 262160 | tf_op jit(solution)/shard_map/reduce_scatter | solution.py:68
  105.5 1.7 copy.23
  107.1 5.0 %all-to-all-start = ((f32[4,64,256]{2,1,0:T(8,128)}), f32[4,64,256]{2,1,0:T(8,128)S(1)}, u32[]{:S(2)}, u32[]{:S(2)}) async-start(f32[4,64,256]{2,1,0:T(8,128)} %bitcast.47), calls=%async_computation.1 | async-start | bytes 524288 | tf_op jit(solution)/shard_map/all_to_all | solution.py:17
  112.1 0.0 copy-done.5
  112.2 5.2 %all-to-all-done = f32[4,64,256]{2,1,0:T(8,128)S(1)} async-done(((f32[4,64,256]{2,1,0:T(8,128)}), f32[4,64,256]{2,1,0:T(8,128)S(1)}, u32[]{:S(2)}, u32[]{:S(2)}) %all-to-all-start) | async-done | bytes 262176 | tf_op jit(solution)/shard_map/all_to_all | solution.py:17
  117.4 3.8 %all_to_all.25 = f32[2,64,128]{2,1,0:T(8,128)S(1)} all-to-all(f32[2,64,128]{2,1,0:T(8,128)S(1)} %copy.13), channel_id=1, replica_groups=mesh['groups'=2,'tp'=16,'tq'=4,'tr'=2] {'tr'}, dimensions={0} | all-to-all | bytes 131072 | tf_op jit(solution)/shard_map/all_to_all | solution.py:17
  121.3 0.0 copy-done.3
  121.3 0.1 fusion.6
  121.4 0.0 copy-start.2
  121.4 27.3 %all-gather.3 = f32[16,2,64]{2,1,0:T(2,128)S(1)} all-gather(f32[1,2,64]{2,1,0:T(2,128)S(1)} %maximum_bitcast_fusion), channel_id=2, replica_groups=mesh['groups'=2,'tp'=16,'tq'=4,'tr'=2] {'tp'}, dimensions={0}, use_global_device_ids=true | all-gather | bytes 8704 | tf_op jit(solution)/shard_map/all_gather | solution.py:29
  148.7 8.5 %all-gather.4 = f32[4,2,64]{2,1,0:T(2,128)S(1)} all-gather(f32[1,2,64]{2,1,0:T(2,128)S(1)} %maximum_bitcast_fusion.1), channel_id=3, replica_groups=mesh['groups'=2,'tp'=16,'tq'=4,'tr'=2] {'tq'}, dimensions={0}, use_global_device_ids=true | all-gather | bytes 2560 | tf_op jit(solution)/shard_map/all_gather | solution.py:29
  157.3 1.9 all-gather.5
  159.1 0.0 copy-start.4
  159.1 0.1 fusion.5
  159.2 3.8 %all_to_all.26 = bf16[2,64,128]{2,1,0:T(8,128)(2,1)S(1)} all-to-all(bf16[2,64,128]{2,1,0:T(8,128)(2,1)S(1)} %broadcast_in_dim.4), channel_id=1, replica_groups=mesh['groups'=2,'tp'=16,'tq'=4,'tr'=2] {'tr'}, dimensions={0} | all-to-all | bytes 65536 | tf_op jit(solution)/shard_map/all_to_all | solution.py:55
  163.0 8.1 %all_to_all.27 = bf16[4,64,256]{2,1,0:T(8,128)(2,1)S(1)} all-to-all(bf16[4,64,256]{2,1,0:T(8,128)(2,1)S(1)} %broadcast_in_dim.5), channel_id=1, replica_groups=mesh['groups'=2,'tp'=16,'tq'=4,'tr'=2] {'tq'}, dimensions={0} | all-to-all | bytes 262144 | tf_op jit(solution)/shard_map/all_to_all | solution.py:55
  171.1 0.3 stack.3
  171.4 0.0 copy-start.1
  171.4 105.6 %all_to_all.28 = bf16[16,64,1024]{2,1,0:T(8,128)(2,1)S(1)} all-to-all(bf16[16,64,1024]{2,1,0:T(8,128)(2,1)S(1)} %stack.3), channel_id=1, replica_groups=mesh['groups'=2,'tp'=16,'tq'=4,'tr'=2] {'tp'}, dimensions={0} | all-to-all | bytes 4194304 | tf_op jit(solution)/shard_map/all_to_all | solution.py:85
  277.0 0.2 copy.20
  277.2 0.0 copy-done.2
  277.3 0.0 copy-done.4
  277.3 0.0 copy-done.1
  277.3 1.5 fusion
  (17 shorter events, 0.2 us)
Async XLA Ops:
  7.2 0.7 copy-start
  7.2 98.3 %reduce-scatter.2.cloned.1.call-start = ((), (), s32[]{:S(2)}) async-start(), calls=%async_computation.6 | async-start | bytes 4456448 | tf_op jit(solution)/shard_map/reduce_scatter | solution.py:68
  12.7 99.4 %copy-start.5 = (bf16[128]{0:T(256)(128)(2,1)S(1)}, bf16[128]{0:T(256)(128)(2,1)}, u32[]{:S(2)}) copy-start(bf16[128]{0:T(256)(128)(2,1)} %param.8) | copy-start | bytes 772
  12.7 108.5 %copy-start.3 = (bf16[64,128]{1,0:T(8,128)(2,1)S(1)}, bf16[64,128]{1,0:T(8,128)(2,1)}, u32[]{:S(2)}) copy-start(bf16[64,128]{1,0:T(8,128)(2,1)} %param.6) | copy-start | bytes 49156
  107.1 10.3 %all-to-all-start = ((f32[4,64,256]{2,1,0:T(8,128)}), f32[4,64,256]{2,1,0:T(8,128)S(1)}, u32[]{:S(2)}, u32[]{:S(2)}) async-start(f32[4,64,256]{2,1,0:T(8,128)} %bitcast.47), calls=%async_computation.1 | async-start | bytes 524288 | tf_op jit(solution)/shard_map/all_to_all | solution.py:17
  121.4 155.9 %copy-start.2 = (bf16[64,128]{1,0:T(8,128)(2,1)}, bf16[64,128]{1,0:T(8,128)(2,1)S(1)}, u32[]{:S(2)}) copy-start(bf16[64,128]{1,0:T(8,128)(2,1)S(1)} %get-tuple-element.8) | copy-start | bytes 49156
  159.1 118.1 %copy-start.4 = (f32[64]{0:T(128)}, f32[64]{0:T(128)S(1)}, u32[]{:S(2)}) copy-start(f32[64]{0:T(128)S(1)} %get-tuple-element.6) | copy-start | bytes 772
  171.4 105.9 %copy-start.1 = (bf16[16384,128]{1,0:T(8,128)(2,1)S(1)}, bf16[16384,128]{1,0:T(8,128)(2,1)}, u32[]{:S(2)}) copy-start(bf16[16384,128]{1,0:T(8,128)(2,1)} %param.9) | copy-start | bytes 12582916
Sparse Core Ops, SparseCore 0:
  12.9 92.5 reduce-scatter.1
